TPU v7x, 32 devices: a whole 2x2x4 slice. The times are simulated.
32 devices in a mesh: fsdp: 2 (over y), trow: 4 (over x, core), tcol: 4 (over z).
Axes of the slice: x: 2, y: 2, z: 4, core: 2. Of those that a mesh axis runs over, the one named last changes fastest.
Arguments:
- tokens: bfloat16 [512, 4096], P('fsdp', 'tcol'), may hold values from -100 to 100
- w_up: bfloat16 [4096, 16384], P('tcol', ('fsdp', 'trow')), may hold values from -0.1875 to 0.1875
- w_down: bfloat16 [16384, 4096], P(('fsdp', 'trow'), 'tcol'), may hold values from -0.046875 to 0.046875
- cotangent: bfloat16 [512, 4096], P('fsdp', 'tcol'), may hold values from -6 to 6
Outputs:
- mixed: bfloat16 [512, 4096], P('fsdp', 'tcol')
- input_gradient: bfloat16 [512, 4096], P('fsdp', 'tcol')
- grad_up: bfloat16 [4096, 16384], P('tcol', ('fsdp', 'trow'))
- grad_down: bfloat16 [16384, 4096], P(('fsdp', 'trow'), 'tcol')
All inputs are finite; a program needn't handle non-finite values.
Results may differ from a plain program's by a relative error of at most 0.02.
Values may be sent and summed in bfloat16 or wider, within the bound.
A program may use at most 128 MiB of HBM per device.

v0:
```python
import jax
import jax.numpy as jnp
from jax import lax
from jax.sharding import PartitionSpec as P


def gelu_value(pre):
    phi = 0.5 * (1.0 + jax.scipy.special.erf(pre * 0.7071067811865476))
    return pre * phi


def gelu_slope(pre):
    phi = 0.5 * (1.0 + jax.scipy.special.erf(pre * 0.7071067811865476))
    return phi + pre * jnp.exp(-0.5 * pre * pre) * 0.3989422804014327


def contract(left, right, left_dim, right_dim):
    return lax.dot_general(
        left, right, (((left_dim,), (right_dim,)), ((), ())), preferred_element_type=jnp.float32
    )


def local(tokens, w_up, w_down, cotangent):
    width = tokens.shape[1] * lax.axis_size("tcol")
    input_float = tokens.astype(jnp.float32)
    sum_one, sum_two = lax.psum(
        (jnp.sum(input_float, axis=1), jnp.sum(input_float * input_float, axis=1)), "tcol"
    )
    token_mean = sum_one / width
    var = sum_two / width - token_mean * token_mean
    inverse_stddev = lax.rsqrt(var + 1e-05)
    centered_scaled = (input_float - token_mean[:, None]) * inverse_stddev[:, None]
    normalized_rows = centered_scaled.astype(jnp.bfloat16)
    up_full, down_full = (
        lax.all_gather(w_up, "fsdp", axis=1, tiled=True),
        lax.all_gather(w_down, "fsdp", axis=0, tiled=True),
    )
    pre_full = lax.psum(
        jnp.dot(normalized_rows, up_full, preferred_element_type=jnp.float32).astype(jnp.bfloat16),
        "tcol",
    ).astype(jnp.float32)
    hidden = gelu_value(pre_full).astype(jnp.bfloat16)
    branch = lax.psum(
        jnp.dot(hidden, down_full, preferred_element_type=jnp.float32).astype(jnp.bfloat16), "trow"
    ).astype(jnp.float32)
    mixed = (input_float + branch).astype(jnp.bfloat16)
    down_part = contract(hidden, cotangent, 0, 0)
    grad_down = lax.psum_scatter(
        down_part.astype(jnp.bfloat16), "fsdp", scatter_dimension=0, tiled=True
    )
    dhid = lax.psum(contract(cotangent, down_full, 1, 1).astype(jnp.bfloat16), "tcol").astype(
        jnp.float32
    )
    dpre = (dhid * gelu_slope(pre_full)).astype(jnp.bfloat16)
    up_part = contract(normalized_rows, dpre, 0, 0)
    grad_up = lax.psum_scatter(
        up_part.astype(jnp.bfloat16), "fsdp", scatter_dimension=1, tiled=True
    )
    normed_gradient = lax.psum(contract(dpre, up_full, 1, 1).astype(jnp.bfloat16), "trow").astype(
        jnp.float32
    )
    mean_first, mean_second = lax.psum(
        (jnp.sum(normed_gradient, axis=1), jnp.sum(normed_gradient * centered_scaled, axis=1)),
        "tcol",
    )
    first_moment = mean_first / width
    second_moment = mean_second / width
    input_gradient = cotangent.astype(jnp.float32) + inverse_stddev[:, None] * (
        normed_gradient - first_moment[:, None] - centered_scaled * second_moment[:, None]
    )
    return (mixed, input_gradient.astype(jnp.bfloat16), grad_up, grad_down)


def solution(mesh):
    return jax.shard_map(
        local,
        mesh=mesh,
        in_specs=(
            P("fsdp", "tcol"),
            P("tcol", ("fsdp", "trow")),
            P(("fsdp", "trow"), "tcol"),
            P("fsdp", "tcol"),
        ),
        out_specs=(
            P("fsdp", "tcol"),
            P("fsdp", "tcol"),
            P("tcol", ("fsdp", "trow")),
            P(("fsdp", "trow"), "tcol"),
        ),
        check_vma=False,
    )
```

profile of v0, /device:TPU:0, one launch (start us, length us, event | category | flops | bytes accessed | tf_op | source)
XLA Modules:
  0.0 644.7 jit_solution(2938886579183394449)
XLA Ops:
  7.2 0.0 all-gather.5.cloned.1.call-start
  7.2 0.7 all-gather.5.cloned.1.call-update
  7.9 0.0 all-gather.3.cloned.1.call-start
  8.0 0.7 all-gather.3.cloned.1.call-update
  8.7 0.0 all-reduce.7.cloned.1.call-start
  8.7 0.2 convert_reduce_fusion
  9.0 13.5 %all-reduce.1 = (f32[256]{0:T(256)S(1)}, f32[256]{0:T(256)S(1)}) all-reduce(f32[256]{0:T(256)S(1)} %get-tuple-element.7, f32[256]{0:T(256)S(1)} %get-tuple-element.6), channel_id=1, replica_groups=mesh['fsdp'=2,'trow'=4,'tcol'=4] {'tcol'}, use_global_device_ids=true, to_apply=%region_3.0 | all-reduce | flops 512 | bytes 4096 | tf_op jit(solution)/shard_map/psum | solution.py:26
  22.5 93.8 %all-gather.5.cloned.1.call-done = bf16[4096,1024]{1,0:T(8,128)(2,1)} async-done(((bf16[2048,1024]{1,0:T(8,128)(2,1)}), bf16[4096,1024]{1,0:T(8,128)(2,1)}) %all-gather.5.cloned.1.call-update) | async-done | bytes 8388624 | tf_op jit(solution)/shard_map/all_gather | solution.py:36
  116.3 7.1 %convolution_convert_fusion.2 = bf16[256,4096]{1,0:T(8,128)(2,1)} fusion(bf16[256,1024]{1,0:T(8,128)(2,1)S(1)} %copy-done.3, bf16[4096,1024]{1,0:T(8,128)(2,1)} %all-gather.5.cloned.1.call-done), kind=kOutput, calls=%fused_computation.7 | convolution fusion | flops 2148532224 | bytes 11010048 | tf_op jit(solution)/shard_map/dot_general | solution.py:18
  123.3 98.5 %all-gather.3.cloned.1.call-done = bf16[1024,4096]{1,0:T(8,128)(2,1)} async-done(((bf16[1024,2048]{1,0:T(8,128)(2,1)}), bf16[1024,4096]{1,0:T(8,128)(2,1)}) %all-gather.3.cloned.1.call-update) | async-done | bytes 8388624 | tf_op jit(solution)/shard_map/all_gather | solution.py:35
  221.8 7.1 %convolution_convert_fusion.3 = bf16[256,4096]{1,0:T(8,128)(2,1)} fusion(bf16[1024,4096]{1,0:T(8,128)(2,1)} %all-gather.3.cloned.1.call-done, bf16[256,1024]{1,0:T(8,128)(2,1)S(1)} %copy-done, f32[256]{0:T(256)S(1)} %get-tuple-element.19, f32[256]{0:T(256)S(1)} %get-tuple-element.18), kind=kOutput, calls=%fused_computation.8 | convolution fusion | flops 2149580800 | bytes 11012096 | tf_op jit(solution)/shard_map/dot_general | solution.py:39
  229.0 0.0 all-reduce.7.cloned.1.call-update
  229.0 0.0 all-reduce.9.cloned.1.call-start
  229.0 155.1 %all-reduce.7.cloned.1.call-done = (bf16[256,4096]{1,0:T(8,128)(2,1)}, bf16[256,4096]{1,0:T(8,128)(2,1)}) async-done(((bf16[256,4096]{1,0:T(8,128)(2,1)}, bf16[256,4096]{1,0:T(8,128)(2,1)}), (bf16[256,4096]{1,0:T(8,128)(2,1)}, bf16[256,4096]{1,0:T(8,128)(2,1)})) %all-reduce.7.cloned.1.call-update) | async-done | bytes 4194320 | tf_op jit(solution)/shard_map/psum | solution.py:38
  384.2 3.7 fusion.8
  387.9 0.0 slice-start.1
  387.9 6.8 %convolution_convert_fusion.5 = bf16[256,1024]{1,0:T(8,128)(2,1)} fusion(bf16[4096,1024]{1,0:T(8,128)(2,1)} %all-gather.5.cloned.1.call-done, bf16[256,4096]{1,0:T(8,128)(2,1)S(1)} %copy-done.1), kind=kOutput, calls=%fused_computation.26 | convolution fusion | flops 2154037248 | bytes 11010048 | tf_op jit(solution)/shard_map/dot_general | solution.py:44
  394.6 3.2 convolution_convert_fusion.4
  397.8 0.0 all-reduce.9.cloned.1.call-update
  397.8 0.2 reduce-scatter.3.cloned.1.call-start
  398.1 5.7 convolution_convert_fusion.1
  403.8 0.0 reduce-scatter.3.cloned.1.call-update
  403.8 0.0 reduce-scatter.5.cloned.1.call-start
  403.9 1.5 copy-done.2
  405.4 4.7 convolution_convert_fusion
  410.1 0.0 reduce-scatter.5.cloned.1.call-update
  410.1 23.2 %all-reduce.9.cloned.1.call-done = (bf16[256,1024]{1,0:T(8,128)(2,1)}, bf16[256,1024]{1,0:T(8,128)(2,1)}) async-done(((bf16[256,1024]{1,0:T(8,128)(2,1)}, bf16[256,1024]{1,0:T(8,128)(2,1)}), (bf16[256,1024]{1,0:T(8,128)(2,1)}, bf16[256,1024]{1,0:T(8,128)(2,1)})) %all-reduce.9.cloned.1.call-update) | async-done | bytes 1048592 | tf_op jit(solution)/shard_map/psum | solution.py:43
  433.3 1.5 convert_reduce_fusion.1
  434.7 11.7 %all-reduce = (f32[256]{0:T(256)S(1)}, f32[256]{0:T(256)S(1)}) all-reduce(f32[256]{0:T(256)S(1)} %get-tuple-element.5, f32[256]{0:T(256)S(1)} %get-tuple-element.4), channel_id=1, replica_groups=mesh['fsdp'=2,'trow'=4,'tcol'=4] {'tcol'}, use_global_device_ids=true, to_apply=%region_11.0 | all-reduce | flops 512 | bytes 4096 | tf_op jit(solution)/shard_map/psum | solution.py:62
  446.4 2.6 fusion.12
  449.0 86.8 %reduce-scatter.3.cloned.1.call-done = bf16[1024,2048]{1,0:T(8,128)(2,1)} async-done(((bf16[1024,4096]{1,0:T(8,128)(2,1)}), bf16[1024,2048]{1,0:T(8,128)(2,1)}) %reduce-scatter.3.cloned.1.call-update) | async-done | bytes 4194320 | tf_op jit(solution)/shard_map/reduce_scatter | solution.py:56
  535.8 102.1 %reduce-scatter.5.cloned.1.call-done = bf16[2048,1024]{1,0:T(8,128)(2,1)} async-done(((bf16[4096,1024]{1,0:T(8,128)(2,1)}), bf16[2048,1024]{1,0:T(8,128)(2,1)}) %reduce-scatter.5.cloned.1.call-update) | async-done | bytes 4194320 | tf_op jit(solution)/shard_map/reduce_scatter | solution.py:48
  (13 shorter events, 0.0 us)
Async XLA Ops:
  7.2 1.6 copy-start
  7.2 109.1 %copy-start.3 = (bf16[256,1024]{1,0:T(8,128)(2,1)S(1)}, bf16[256,1024]{1,0:T(8,128)(2,1)}, u32[]{:S(2)}) copy-start(bf16[256,1024]{1,0:T(8,128)(2,1)} %param.7) | copy-start | bytes 1572868
  7.2 109.1 %all-gather.5.cloned.1.call-start = ((), (), s32[]{:S(2)}) async-start(), calls=%async_computation.3 | async-start | bytes 12582912 | tf_op jit(solution)/shard_map/all_gather | solution.py:36
  7.9 213.9 %all-gather.3.cloned.1.call-start = ((), (), s32[]{:S(2)}) async-start(), calls=%async_computation.2 | async-start | bytes 12582912 | tf_op jit(solution)/shard_map/all_gather | solution.py:35
  8.7 375.5 %all-reduce.7.cloned.1.call-start = ((), (), s32[]{:S(2)}) async-start(), calls=%async_computation.6 | async-start | bytes 8388608 | tf_op jit(solution)/shard_map/psum | solution.py:38
  229.0 204.3 %all-reduce.9.cloned.1.call-start = ((), (), s32[]{:S(2)}) async-start(), calls=%async_computation.7 | async-start | bytes 2097152 | tf_op jit(solution)/shard_map/psum | solution.py:43
  384.2 3.7 copy-start.1
  384.2 10.5 %slice-start = ((s8[8388608]{0:T(1024)(128)(4,1)}), s8[4194304]{0:T(1024)(128)(4,1)S(1)}, s32[]{:S(2)}) async-start(s8[8388608]{0:T(1024)(128)(4,1)} %bitcast.8), calls=%async_computation.8 | async-start | bytes 8388608
  387.9 6.8 %slice-start.1 = ((s8[8388608]{0:T(1024)(128)(4,1)}), s8[4194304]{0:T(1024)(128)(4,1)S(1)}, s32[]{:S(2)}) async-start(s8[8388608]{0:T(1024)(128)(4,1)} %bitcast.8), calls=%async_computation.9 | async-start | bytes 8388608
  397.8 138.0 %reduce-scatter.3.cloned.1.call-start = ((), (), s32[]{:S(2)}) async-start(), calls=%async_computation.4 | async-start | bytes 12582912 | tf_op jit(solution)/shard_map/reduce_scatter | solution.py:56
  403.8 1.6 copy-start.2
  403.8 234.1 %reduce-scatter.5.cloned.1.call-start = ((), (), s32[]{:S(2)}) async-start(), calls=%async_computation.5 | async-start | bytes 12582912 | tf_op jit(solution)/shard_map/reduce_scatter | solution.py:48
Sparse Core Ops, SparseCore 0:
  9.5 106.6 all-gather.4
  117.8 103.9 all-gather.2
  229.1 155.0 all-reduce.6
  398.0 35.2 all-reduce.8
  436.0 99.7 reduce-scatter.2
  538.6 99.2 reduce-scatter.4
where the time goes:
time: 645 us
  waiting for transfers between devices  561 us (87%)
  matrix products  34.6 us (5%)
  blocking collectives  25.2 us (4%)
  between operations  14.2 us (2%)
  other arithmetic  7.98 us (1%)
    psum x1, waiting for transfers between devices, local(): lax.psum(jnp.dot(normalized_rows, up_full, preferred_element_type=jnp.flo...  155 us
    reduce_scatter x1, waiting for transfers between devices, local(): lax.psum_scatter(down_part.astype(jnp.bfloat16), 'fsdp', scatter_dimensio...  102 us
    all_gather x1, waiting for transfers between devices, local(): lax.all_gather(w_up, 'fsdp', axis=1, tiled=True)  98.5 us
    all_gather x1, waiting for transfers between devices, local(): lax.all_gather(w_down, 'fsdp', axis=0, tiled=True)  93.8 us
    reduce_scatter x1, waiting for transfers between devices, local(): lax.psum_scatter(up_part.astype(jnp.bfloat16), 'fsdp', scatter_dimension=...  86.8 us
    psum x1, waiting for transfers between devices, local(): lax.psum(jnp.dot(hidden, down_full, preferred_element_type=jnp.float32).a...  23.2 us
    dot_general x4, matrix products, contract(): lax.dot_general(left, right, (((left_dim,), (right_dim,)), ((), ())), pre...  20.7 us
    psum x1, blocking collectives, local(): lax.psum((jnp.sum(input_float, axis=1), jnp.sum(input_float * input_float...  13.5 us
  transfers between devices with their start and end apart: 6, of which 6 were waited for; matrix products, arithmetic and copies ran while one was open for 3% of the time, Pallas kernels for 0%

commit v1 on v0

--- a/solution.py
+++ b/solution.py
@@ -23,6 +23,7 @@
 def local(tokens, w_up, w_down, cotangent):
     width = tokens.shape[1] * lax.axis_size("tcol")
     input_float = tokens.astype(jnp.float32)
+    cot_all = lax.all_gather(cotangent, "fsdp", axis=0, tiled=True)
     sum_one, sum_two = lax.psum(
         (jnp.sum(input_float, axis=1), jnp.sum(input_float * input_float, axis=1)), "tcol"
     )
@@ -31,34 +32,24 @@
     inverse_stddev = lax.rsqrt(var + 1e-05)
     centered_scaled = (input_float - token_mean[:, None]) * inverse_stddev[:, None]
     normalized_rows = centered_scaled.astype(jnp.bfloat16)
-    up_full, down_full = (
-        lax.all_gather(w_up, "fsdp", axis=1, tiled=True),
-        lax.all_gather(w_down, "fsdp", axis=0, tiled=True),
+    normed_all = lax.all_gather(normalized_rows, "fsdp", axis=0, tiled=True)
+    dhid_part = contract(cot_all, w_down, 1, 1).astype(jnp.bfloat16)
+    dhid = lax.psum_scatter(dhid_part, "tcol", scatter_dimension=0, tiled=True).astype(jnp.float32)
+    pre_part = contract(normed_all, w_up, 1, 0).astype(jnp.bfloat16)
+    pre = lax.psum_scatter(pre_part, "tcol", scatter_dimension=0, tiled=True).astype(jnp.float32)
+    hidden = lax.all_gather(gelu_value(pre).astype(jnp.bfloat16), "tcol", axis=0, tiled=True)
+    dpre = lax.all_gather(
+        (dhid * gelu_slope(pre)).astype(jnp.bfloat16), "tcol", axis=0, tiled=True
     )
-    pre_full = lax.psum(
-        jnp.dot(normalized_rows, up_full, preferred_element_type=jnp.float32).astype(jnp.bfloat16),
-        "tcol",
-    ).astype(jnp.float32)
-    hidden = gelu_value(pre_full).astype(jnp.bfloat16)
-    branch = lax.psum(
-        jnp.dot(hidden, down_full, preferred_element_type=jnp.float32).astype(jnp.bfloat16), "trow"
-    ).astype(jnp.float32)
+    branch_part = contract(hidden, w_down, 1, 0).astype(jnp.bfloat16)
+    branch = lax.psum_scatter(branch_part, "fsdp", scatter_dimension=0, tiled=True)
+    branch = lax.psum(branch, "trow").astype(jnp.float32)
     mixed = (input_float + branch).astype(jnp.bfloat16)
-    down_part = contract(hidden, cotangent, 0, 0)
-    grad_down = lax.psum_scatter(
-        down_part.astype(jnp.bfloat16), "fsdp", scatter_dimension=0, tiled=True
-    )
-    dhid = lax.psum(contract(cotangent, down_full, 1, 1).astype(jnp.bfloat16), "tcol").astype(
-        jnp.float32
-    )
-    dpre = (dhid * gelu_slope(pre_full)).astype(jnp.bfloat16)
-    up_part = contract(normalized_rows, dpre, 0, 0)
-    grad_up = lax.psum_scatter(
-        up_part.astype(jnp.bfloat16), "fsdp", scatter_dimension=1, tiled=True
-    )
-    normed_gradient = lax.psum(contract(dpre, up_full, 1, 1).astype(jnp.bfloat16), "trow").astype(
-        jnp.float32
-    )
+    grad_down = contract(hidden, cot_all, 0, 0).astype(jnp.bfloat16)
+    dnorm_part = contract(dpre, w_up, 1, 1).astype(jnp.bfloat16)
+    dnorm = lax.psum_scatter(dnorm_part, "fsdp", scatter_dimension=0, tiled=True)
+    normed_gradient = lax.psum(dnorm, "trow").astype(jnp.float32)
+    grad_up = contract(normed_all, dpre, 0, 0).astype(jnp.bfloat16)
     mean_first, mean_second = lax.psum(
         (jnp.sum(normed_gradient, axis=1), jnp.sum(normed_gradient * centered_scaled, axis=1)),
         "tcol",

time: 645 us -> 360 us (0.56)
  waiting for transfers between devices: 561 us -> 276 us
    psum x2 -> x1, waiting for transfers between devices: 178 us -> 29.9 us  [local(): branch = lax.psum(branch, 'trow').astype(jnp.float32)]
    all_gather x2 -> x4, waiting for transfers between devices: 192 us -> 120 us  [the longest x1 44.4 us: local(): lax.all_gather(gelu_value(pre).astype(jnp.bfloat16), 'tcol', axis=0, tile...]
    reduce_scatter x2 -> x4, waiting for transfers between devices: 189 us -> 125 us  [the longest x1 45.6 us: local(): lax.psum_scatter(dhid_part, 'tcol', scatter_dimension=0, tiled=True)]
    dot_general x2 -> x0, matrix products: 13.9 us -> none  [the longest x1 7.13 us: local(): jnp.dot(normalized_rows, up_full, preferred_element_type=jnp.float32)]
    dot_general x4 -> x6, matrix products: 20.7 us -> 33.5 us  [contract(): lax.dot_general(left, right, (((left_dim,), (right_dim,)), ((), ())), pre...]
  transfers between devices with their start and end apart: 6 -> 9, of which waited for: 6 -> 9; matrix products, arithmetic and copies ran while one was open for 3% -> 9% of each run, Pallas kernels for 0% -> 0%
where the time goes in v1:
time: 360 us; the launch traced here: 359 us
  waiting for transfers between devices  276 us (77%)
  matrix products  33.5 us (9%)
  blocking collectives  25.2 us (7%)
  between operations  13.9 us (4%)
  other arithmetic  10.2 us (3%)
    reduce_scatter x1, waiting for transfers between devices, local(): lax.psum_scatter(dhid_part, 'tcol', scatter_dimension=0, tiled=True)  45.6 us
    all_gather x1, waiting for transfers between devices, local(): lax.all_gather(gelu_value(pre).astype(jnp.bfloat16), 'tcol', axis=0, tile...  44.4 us
    all_gather x1, waiting for transfers between devices, local(): lax.all_gather((dhid * gelu_slope(pre)).astype(jnp.bfloat16), 'tcol', axi...  40.3 us
    reduce_scatter x1, waiting for transfers between devices, local(): lax.psum_scatter(pre_part, 'tcol', scatter_dimension=0, tiled=True)  40.3 us
    dot_general x6, matrix products, contract(): lax.dot_general(left, right, (((left_dim,), (right_dim,)), ((), ())), pre...  33.5 us
    psum x1, waiting for transfers between devices, local(): branch = lax.psum(branch, 'trow').astype(jnp.float32)  29.9 us
    reduce_scatter x1, waiting for transfers between devices, local(): lax.psum_scatter(dnorm_part, 'fsdp', scatter_dimension=0, tiled=True)  23.2 us
    all_gather x1, waiting for transfers between devices, local(): normed_all = lax.all_gather(normalized_rows, 'fsdp', axis=0, tiled=True)  18.9 us
  transfers between devices with their start and end apart: 9, of which 9 were waited for; matrix products, arithmetic and copies ran while one was open for 9% of the time, Pallas kernels for 0%

profile of v1, /device:TPU:0, one launch (start us, length us, event | category | flops | bytes accessed | tf_op | source)
XLA Modules:
  0.0 359.4 jit_solution(15157938787356180238)
XLA Ops:
  7.2 0.0 all-gather.5.cloned.1.call-start
  7.2 1.3 convert_reduce_fusion
  8.5 13.5 %all-reduce.1 = (f32[256]{0:T(256)S(1)}, f32[256]{0:T(256)S(1)}) all-reduce(f32[256]{0:T(256)S(1)} %get-tuple-element.7, f32[256]{0:T(256)S(1)} %get-tuple-element.6), channel_id=1, replica_groups=mesh['fsdp'=2,'trow'=4,'tcol'=4] {'tcol'}, use_global_device_ids=true, to_apply=%region_3.0 | all-reduce | flops 512 | bytes 4096 | tf_op jit(solution)/shard_map/psum | solution.py:27
  22.0 2.1 fusion.7
  24.1 0.0 all-gather.9.cloned.1.call-start
  24.2 0.7 all-gather.9.cloned.1.call-update
  24.9 18.9 %all-gather.5.cloned.1.call-done = bf16[512,1024]{1,0:T(8,128)(2,1)} async-done(((bf16[256,1024]{1,0:T(8,128)(2,1)}), bf16[512,1024]{1,0:T(8,128)(2,1)}) %all-gather.5.cloned.1.call-update) | async-done | bytes 1048592 | tf_op jit(solution)/shard_map/all_gather | solution.py:35
  43.8 6.2 %convolution_convert_fusion.3 = bf16[512,2048]{1,0:T(8,128)(2,1)} fusion(bf16[512,1024]{1,0:T(8,128)(2,1)} %all-gather.5.cloned.1.call-done, bf16[1024,2048]{1,0:T(8,128)(2,1)} %param.5), kind=kOutput, calls=%fused_computation.3 | convolution fusion | flops 2148532224 | bytes 7340032 | tf_op jit(solution)/shard_map/dot_general | solution.py:18
  49.9 0.0 reduce-scatter.9.cloned.1.call-start
  50.0 16.6 %all-gather.9.cloned.1.call-done = bf16[512,1024]{1,0:T(8,128)(2,1)} async-done(((bf16[256,1024]{1,0:T(8,128)(2,1)}), bf16[512,1024]{1,0:T(8,128)(2,1)}) %all-gather.9.cloned.1.call-update) | async-done | bytes 1048592 | tf_op jit(solution)/shard_map/all_gather | solution.py:26
  66.6 6.2 %convolution_convert_fusion.2 = bf16[512,2048]{1,0:T(8,128)(2,1)} fusion(bf16[512,1024]{1,0:T(8,128)(2,1)} %all-gather.9.cloned.1.call-done, bf16[2048,1024]{1,0:T(8,128)(2,1)} %param.6), kind=kOutput, calls=%fused_computation.2 | convolution fusion | flops 2148532224 | bytes 7340032 | tf_op jit(solution)/shard_map/dot_general | solution.py:18
  72.8 0.0 all-gather.7.cloned.1.call-start
  72.9 40.3 %reduce-scatter.5.cloned.1.call-done = bf16[128,2048]{1,0:T(8,128)(2,1)} async-done(((bf16[512,2048]{1,0:T(8,128)(2,1)}), bf16[128,2048]{1,0:T(8,128)(2,1)}) %reduce-scatter.5.cloned.1.call-update) | async-done | bytes 524304 | tf_op jit(solution)/shard_map/reduce_scatter | solution.py:39
  113.2 45.6 %reduce-scatter.9.cloned.1.call-done = bf16[128,2048]{1,0:T(8,128)(2,1)} async-done(((bf16[512,2048]{1,0:T(8,128)(2,1)}), bf16[128,2048]{1,0:T(8,128)(2,1)}) %reduce-scatter.9.cloned.1.call-update) | async-done | bytes 524304 | tf_op jit(solution)/shard_map/reduce_scatter | solution.py:37
  158.7 2.7 fusion.18
  161.5 0.0 all-gather.11.cloned.1.call-start
  161.5 0.5 all-gather.11.cloned.1.call-update
  162.0 0.0 reduce-scatter.7.cloned.1.call-start
  162.1 44.4 %all-gather.7.cloned.1.call-done = bf16[512,2048]{1,0:T(8,128)(2,1)} async-done(((bf16[128,2048]{1,0:T(8,128)(2,1)}), bf16[512,2048]{1,0:T(8,128)(2,1)}) %all-gather.7.cloned.1.call-update) | async-done | bytes 2097168 | tf_op jit(solution)/shard_map/all_gather | solution.py:40
  206.5 6.1 %convolution_convert_fusion.5 = bf16[512,1024]{1,0:T(8,128)(2,1)} fusion(bf16[512,2048]{1,0:T(8,128)(2,1)} %all-gather.7.cloned.1.call-done, bf16[2048,1024]{1,0:T(8,128)(2,1)} %param.6), kind=kOutput, calls=%fused_computation.17 | convolution fusion | flops 2148007936 | bytes 7340032 | tf_op jit(solution)/shard_map/dot_general | solution.py:18
  212.6 0.0 reduce-scatter.11.cloned.1.call-start
  212.7 40.3 %all-gather.11.cloned.1.call-done = bf16[512,2048]{1,0:T(8,128)(2,1)} async-done(((bf16[128,2048]{1,0:T(8,128)(2,1)}), bf16[512,2048]{1,0:T(8,128)(2,1)}) %all-gather.11.cloned.1.call-update) | async-done | bytes 2097168 | tf_op jit(solution)/shard_map/all_gather | solution.py:41
  253.0 6.2 %convolution_convert_fusion.4 = bf16[512,1024]{1,0:T(8,128)(2,1)} fusion(bf16[512,2048]{1,0:T(8,128)(2,1)} %all-gather.11.cloned.1.call-done, bf16[1024,2048]{1,0:T(8,128)(2,1)} %param.5), kind=kOutput, calls=%fused_computation.16 | convolution fusion | flops 2148007936 | bytes 7340032 | tf_op jit(solution)/shard_map/dot_general | solution.py:18
  259.1 0.2 all-reduce.5.cloned.1.call-start
  259.4 15.6 %reduce-scatter.7.cloned.1.call-done = bf16[256,1024]{1,0:T(8,128)(2,1)} async-done(((bf16[512,1024]{1,0:T(8,128)(2,1)}), bf16[256,1024]{1,0:T(8,128)(2,1)}) %reduce-scatter.7.cloned.1.call-update) | async-done | bytes 524304 | tf_op jit(solution)/shard_map/reduce_scatter | solution.py:45
  275.0 23.2 %reduce-scatter.11.cloned.1.call-done = bf16[256,1024]{1,0:T(8,128)(2,1)} async-done(((bf16[512,1024]{1,0:T(8,128)(2,1)}), bf16[256,1024]{1,0:T(8,128)(2,1)}) %reduce-scatter.11.cloned.1.call-update) | async-done | bytes 524304 | tf_op jit(solution)/shard_map/reduce_scatter | solution.py:50
  298.3 4.4 %convolution_convert_fusion = bf16[2048,1024]{1,0:T(8,128)(2,1)} fusion(bf16[512,2048]{1,0:T(8,128)(2,1)S(1)} %copy-done.2, bf16[512,1024]{1,0:T(8,128)(2,1)S(1)} %copy-done.5), kind=kOutput, calls=%fused_computation | convolution fusion | flops 2149580800 | bytes 7340032 | tf_op jit(solution)/shard_map/dot_general | solution.py:18
  302.7 4.4 %convolution_convert_fusion.1 = bf16[1024,2048]{1,0:T(8,128)(2,1)} fusion(bf16[512,1024]{1,0:T(8,128)(2,1)S(1)} %copy-done.4, bf16[512,2048]{1,0:T(8,128)(2,1)S(1)} %copy-done.3), kind=kOutput, calls=%fused_computation.1 | convolution fusion | flops 2149580800 | bytes 7340032 | tf_op jit(solution)/shard_map/dot_general | solution.py:18
  307.2 29.9 %all-reduce.5.cloned.1.call-done = (bf16[256,1024]{1,0:T(8,128)(2,1)}, bf16[256,1024]{1,0:T(8,128)(2,1)}) async-done(((bf16[256,1024]{1,0:T(8,128)(2,1)}, bf16[256,1024]{1,0:T(8,128)(2,1)}), (bf16[256,1024]{1,0:T(8,128)(2,1)}, bf16[256,1024]{1,0:T(8,128)(2,1)})) %all-reduce.5.cloned.1.call-update) | async-done | bytes 1048592 | tf_op jit(solution)/shard_map/psum | solution.py:46
  337.1 1.5 convert_reduce_fusion.1
  338.5 11.7 %all-reduce = (f32[256]{0:T(256)S(1)}, f32[256]{0:T(256)S(1)}) all-reduce(f32[256]{0:T(256)S(1)} %get-tuple-element.5, f32[256]{0:T(256)S(1)} %get-tuple-element.4), channel_id=1, replica_groups=mesh['fsdp'=2,'trow'=4,'tcol'=4] {'tcol'}, use_global_device_ids=true, to_apply=%region_13.0 | all-reduce | flops 512 | bytes 4096 | tf_op jit(solution)/shard_map/psum | solution.py:53
  350.2 2.6 fusion.3
  (22 shorter events, 0.2 us)
Async XLA Ops:
  7.2 36.6 %all-gather.5.cloned.1.call-start = ((), (), s32[]{:S(2)}) async-start(), calls=%async_computation.4 | async-start | bytes 1572864 | tf_op jit(solution)/shard_map/all_gather | solution.py:35
  24.1 42.5 %all-gather.9.cloned.1.call-start = ((), (), s32[]{:S(2)}) async-start(), calls=%async_computation.8 | async-start | bytes 1572864 | tf_op jit(solution)/shard_map/all_gather | solution.py:26
  24.9 88.3 %reduce-scatter.5.cloned.1.call-start = ((), (), s32[]{:S(2)}) async-start(), calls=%async_computation.5 | async-start | bytes 2621440 | tf_op jit(solution)/shard_map/reduce_scatter | solution.py:39
  49.9 108.8 %reduce-scatter.9.cloned.1.call-start = ((), (), s32[]{:S(2)}) async-start(), calls=%async_computation.9 | async-start | bytes 2621440 | tf_op jit(solution)/shard_map/reduce_scatter | solution.py:37
  72.8 133.6 %all-gather.7.cloned.1.call-start = ((), (), s32[]{:S(2)}) async-start(), calls=%async_computation.6 | async-start | bytes 2621440 | tf_op jit(solution)/shard_map/all_gather | solution.py:40
  161.5 91.5 %all-gather.11.cloned.1.call-start = ((), (), s32[]{:S(2)}) async-start(), calls=%async_computation.10 | async-start | bytes 2621440 | tf_op jit(solution)/shard_map/all_gather | solution.py:41
  162.0 113.0 %reduce-scatter.7.cloned.1.call-start = ((), (), s32[]{:S(2)}) async-start(), calls=%async_computation.7 | async-start | bytes 1572864 | tf_op jit(solution)/shard_map/reduce_scatter | solution.py:45
  212.6 85.6 %copy-start.2 = (bf16[512,2048]{1,0:T(8,128)(2,1)S(1)}, bf16[512,2048]{1,0:T(8,128)(2,1)}, u32[]{:S(2)}) copy-start(bf16[512,2048]{1,0:T(8,128)(2,1)} %all-gather.7.cloned.1.call-done) | copy-start | bytes 6291460
  212.6 85.6 %copy-start.5 = (bf16[512,1024]{1,0:T(8,128)(2,1)S(1)}, bf16[512,1024]{1,0:T(8,128)(2,1)}, u32[]{:S(2)}) copy-start(bf16[512,1024]{1,0:T(8,128)(2,1)} %all-gather.9.cloned.1.call-done) | copy-start | bytes 3145732
  212.6 85.6 %reduce-scatter.11.cloned.1.call-start = ((), (), s32[]{:S(2)}) async-start(), calls=%async_computation.11 | async-start | bytes 1572864 | tf_op jit(solution)/shard_map/reduce_scatter | solution.py:50
  259.1 77.9 %all-reduce.5.cloned.1.call-start = ((), (), s32[]{:S(2)}) async-start(), calls=%async_computation.12 | async-start | bytes 2097152 | tf_op jit(solution)/shard_map/psum | solution.py:46
  298.3 4.4 %copy-start.3 = (bf16[512,2048]{1,0:T(8,128)(2,1)S(1)}, bf16[512,2048]{1,0:T(8,128)(2,1)}, u32[]{:S(2)}) copy-start(bf16[512,2048]{1,0:T(8,128)(2,1)} %all-gather.11.cloned.1.call-done) | copy-start | bytes 6291460
  298.3 4.4 %copy-start.4 = (bf16[512,1024]{1,0:T(8,128)(2,1)S(1)}, bf16[512,1024]{1,0:T(8,128)(2,1)}, u32[]{:S(2)}) copy-start(bf16[512,1024]{1,0:T(8,128)(2,1)} %all-gather.5.cloned.1.call-done) | copy-start | bytes 3145732
  302.7 34.3 %copy-start = (bf16[256,1024]{1,0:T(8,128)(2,1)S(1)}, bf16[256,1024]{1,0:T(8,128)(2,1)}, u32[]{:S(2)}) copy-start(bf16[256,1024]{1,0:T(8,128)(2,1)} %param.4) | copy-start | bytes 1572868
  302.7 47.5 %copy-start.1 = (bf16[256,1024]{1,0:T(8,128)(2,1)S(1)}, bf16[256,1024]{1,0:T(8,128)(2,1)}, u32[]{:S(2)}) copy-start(bf16[256,1024]{1,0:T(8,128)(2,1)} %param.7) | copy-start | bytes 1572868
Sparse Core Ops, SparseCore 0:
  24.2 19.4 all-gather.4
  45.3 21.2 all-gather.8
  69.5 43.6 reduce-scatter.4
  115.9 42.8 reduce-scatter.8
  161.6 44.8 all-gather.6
  208.5 44.4 all-gather.10
  255.8 19.1 reduce-scatter.6
  277.8 20.3 reduce-scatter.10
  300.7 36.3 all-reduce.4

commit v2 on v1

--- a/solution.py
+++ b/solution.py
@@ -1,16 +1,20 @@
+import functools
+
 import jax
 import jax.numpy as jnp
 from jax import lax
+from jax.experimental import pallas as pl
+from jax.experimental.pallas import tpu as pltpu
 from jax.sharding import PartitionSpec as P
 
 
 def gelu_value(pre):
-    phi = 0.5 * (1.0 + jax.scipy.special.erf(pre * 0.7071067811865476))
+    phi = 0.5 * (1.0 + lax.erf(pre * 0.7071067811865476))
     return pre * phi
 
 
 def gelu_slope(pre):
-    phi = 0.5 * (1.0 + jax.scipy.special.erf(pre * 0.7071067811865476))
+    phi = 0.5 * (1.0 + lax.erf(pre * 0.7071067811865476))
     return phi + pre * jnp.exp(-0.5 * pre * pre) * 0.3989422804014327
 
 
@@ -62,9 +66,409 @@
     return (mixed, input_gradient.astype(jnp.bfloat16), grad_up, grad_down)
 
 
+MESH = pl.DeviceIdType.MESH
+BF, F32 = jnp.bfloat16, jnp.float32
+
+
+def block_kernel(
+    F, R, P, tok, cot, wup_h, wdn_h, mix_h, ig_h, nrm_h, cota_h, hid_h, dpr_h,
+    wup, wdn, nrm, cota, hid, dpr, part, rec_r, rec_l, acc, slope, ybuf, xrec, mix, ig, dn,
+    mean_s, rstd_s, st1, st2,
+    load_sem, out_sem, ys, yr, st_s, st_r, fr_s, fr_r, fl_s, fl_r, ag_rs, ag_ls, ag_r, xs, xr, ms, mr,
+):
+    T, W = tok.shape
+    H = wdn.shape[0]
+    TC, TR = T // P, T // R
+    K = 2 * F
+    f, rr, p = lax.axis_index("fsdp"), lax.axis_index("trow"), lax.axis_index("tcol")
+    sends = []
+
+    barrier = pltpu.get_barrier_semaphore()
+    for g in range(F):
+        for j in range(R):
+            if g or j:
+                pl.semaphore_signal(
+                    barrier,
+                    inc=1,
+                    device_id={"fsdp": lax.rem(f + g, F), "trow": lax.rem(rr + j, R)},
+                    device_id_type=MESH,
+                )
+    for j in range(1, P):
+        pl.semaphore_signal(
+            barrier, inc=1, device_id={"tcol": lax.rem(p + j, P)}, device_id_type=MESH
+        )
+    loads = [
+        pltpu.make_async_copy(wup_h, wup, load_sem.at[0]),
+        pltpu.make_async_copy(wdn_h, wdn, load_sem.at[1]),
+    ]
+    for copy in loads:
+        copy.start()
+
+    def group(g):
+        return lax.rem(f + g, F)
+
+    def rows(g):
+        return pl.ds(pl.multiple_of(group(g) * T, T), T)
+
+    def chunk(g, c):
+        return pl.ds(pl.multiple_of(group(g) * T + c * TC, TC), TC)
+
+    def remote(src, dst, s, r, to):
+        return pltpu.make_async_remote_copy(
+            src_ref=src, dst_ref=dst, send_sem=s, recv_sem=r, device_id=to, device_id_type=MESH
+        )
+
+    def share(buf, m, g):
+        return remote(
+            buf.at[rows(0), :], buf.at[rows(0), :], ys.at[m, g], yr.at[m, g], {"fsdp": group(g)}
+        )
+
+    def arrive(buf, m, g):
+        src = lax.rem(f + F - g, F)
+        there = pl.ds(pl.multiple_of(src * T, T), T)
+        remote(
+            buf.at[there, :], buf.at[there, :], ys.at[m, g], yr.at[m, g], {"fsdp": group(g)}
+        ).wait_recv()
+
+    cota[rows(0), :] = cot[...]
+    x = tok[...].astype(F32)
+    s1 = jnp.sum(x, axis=1, keepdims=True)
+    s2 = jnp.sum(x * x, axis=1, keepdims=True)
+    lane = lax.broadcasted_iota(jnp.int32, (T, 128), 1)
+    st1[0] = jnp.where(lane == 0, s1, jnp.where(lane == 1, s2, 0.0)).T[:8]
+    pl.semaphore_wait(barrier, F * R - 1 + P - 1)
+
+    def stat(buf, m, j):
+        return remote(
+            buf.at[0], buf.at[j], st_s.at[m, j], st_r.at[m, j], {"tcol": lax.rem(p + j, P)}
+        )
+
+    for j in range(1, P):
+        stat(st1, 0, j).start()
+    for g in range(1, F):
+        share(cota, 1, g).start()
+    total = st1[0]
+    for j in range(1, P):
+        stat(st1, 0, j).wait_recv()
+        total = total + st1[j]
+    width = W * P
+    total = total.T
+    mean = total[:, 0:1] / width
+    var = total[:, 1:2] / width - mean * mean
+    rstd = lax.rsqrt(var + 1e-05)
+    mean_s[...] = jnp.broadcast_to(mean, mean_s.shape)
+    rstd_s[...] = jnp.broadcast_to(rstd, rstd_s.shape)
+    nrm[rows(0), :] = ((tok[...].astype(F32) - mean) * rstd).astype(BF)
+    for g in range(1, F):
+        share(nrm, 0, g).start()
+
+    BN = min(H, 512)
+
+    def partial(k):
+        g, m = k // 2, k % 2
+        if g:
+            arrive((nrm, cota)[m], m, F - g)
+
+        def body(i, _):
+            n = pl.ds(pl.multiple_of(i * BN, BN), BN)
+            if m == 0:
+                out = jnp.dot(nrm[rows(g), :], wup[:, n], preferred_element_type=F32)
+            else:
+                out = contract(cota[rows(g), :], wdn[n, :], 1, 1)
+            part[k, :, n] = out.astype(BF)
+            return 0
+
+        lax.fori_loop(0, H // BN, body, 0)
+
+    def at(c):
+        return pl.ds(pl.multiple_of(c * TC, TC), TC)
+
+    def to_right(k, c):
+        return remote(
+            part.at[k, at(c), :], rec_r.at[k, c], fr_s.at[k, c], fr_r.at[k, c],
+            {"tcol": lax.rem(p + 1, P)},
+        )
+
+    def to_left(k, c):
+        return remote(
+            part.at[k, at(c), :], rec_l.at[k, c], fl_s.at[k, c], fl_r.at[k, c],
+            {"tcol": lax.rem(p + P - 1, P)},
+        )
+
+    def add(k, c, rec):
+        part[k, at(c), :] = (
+            part[k, at(c), :].astype(F32) + rec[k, c].astype(F32)
+        ).astype(BF)
+
+    def flow(k, t):
+        @pl.when(p <= t)
+        def _():
+            c = P - 1 - t + p
+
+            @pl.when(p > 0)
+            def _():
+                to_right(k, c).wait_recv()
+                add(k, c, rec_r)
+
+            to_right(k, c).start()
+
+        @pl.when(p >= P - 1 - t)
+        def _():
+            c = t - P + 1 + p
+
+            @pl.when(p < P - 1)
+            def _():
+                to_left(k, c).wait_recv()
+                add(k, c, rec_l)
+
+            to_left(k, c).start()
+
+    def flow_end(k, t):
+        @pl.when(p <= t)
+        def _():
+            to_right(k, P - 1 - t + p).wait_send()
+
+        @pl.when(p >= P - 1 - t)
+        def _():
+            to_left(k, t - P + 1 + p).wait_send()
+
+    def final(k):
+        g, m = k // 2, k % 2
+        acc[...] = part[k, at(p), :].astype(F32)
+
+        @pl.when(p > 0)
+        def _():
+            to_right(k, p).wait_recv()
+            acc[...] += rec_r[k, p].astype(F32)
+
+        @pl.when(p < P - 1)
+        def _():
+            to_left(k, p).wait_recv()
+            acc[...] += rec_l[k, p].astype(F32)
+
+        def body(i, _):
+            n = pl.ds(pl.multiple_of(i * BN, BN), BN)
+            a = acc[:, n]
+            if m == 0:
+                hid[chunk(g, p), n] = gelu_value(a).astype(BF)
+                slope[:, n] = gelu_slope(a)
+            else:
+                dpr[chunk(g, p), n] = (a * slope[:, n]).astype(BF)
+            return 0
+
+        lax.fori_loop(0, H // BN, body, 0)
+
+    def pass_right(k, c):
+        buf = (hid, dpr)[k % 2].at[chunk(k // 2, c), :]
+        return remote(buf, buf, ag_rs.at[k, c], ag_r.at[k, c], {"tcol": lax.rem(p + 1, P)})
+
+    def pass_left(k, c):
+        buf = (hid, dpr)[k % 2].at[chunk(k // 2, c), :]
+        return remote(buf, buf, ag_ls.at[k, c], ag_r.at[k, c], {"tcol": lax.rem(p + P - 1, P)})
+
+    def spread(k, d):
+        def right():
+            if d:
+                pass_right(k, p - d).wait_recv()
+
+            @pl.when(p < P - 1)
+            def _():
+                pass_right(k, p - d).start()
+
+        def left():
+            if d:
+                pass_left(k, p + d).wait_recv()
+
+            @pl.when(p > 0)
+            def _():
+                pass_left(k, p + d).start()
+
+        pl.when(p >= d)(right)
+        pl.when(p + d <= P - 1)(left)
+
+    def spread_end(k, d):
+        @pl.when((p >= d) & (p < P - 1))
+        def _():
+            pass_right(k, p - d).wait_send()
+
+        @pl.when((p + d <= P - 1) & (p > 0))
+        def _():
+            pass_left(k, p + d).wait_send()
+
+    def piece(k, j):
+        g, m = k // 2, k % 2
+        r = lax.rem(rr + j, R)
+        return remote(
+            ybuf.at[k, pl.ds(pl.multiple_of(r * TR, TR), TR), :], xrec.at[m, g, j],
+            xs.at[m, g, j], xr.at[m, g, j], {"fsdp": group(g), "trow": r},
+        )
+
+    BW = min(W, 256)
+
+    def consume(k):
+        g, m = k // 2, k % 2
+
+        def body(i, _):
+            n = pl.ds(pl.multiple_of(i * BW, BW), BW)
+            if m == 0:
+                out = jnp.dot(hid[rows(g), :], wdn[:, n], preferred_element_type=F32)
+            else:
+                out = contract(dpr[rows(g), :], wup[n, :], 1, 1)
+            ybuf[k, :, n] = out.astype(BF)
+            return 0
+
+        lax.fori_loop(0, W // BW, body, 0)
+        for j in range(R):
+            if g or j:
+                piece(k, j).start()
+
+    mine = pl.ds(pl.multiple_of(rr * TR, TR), TR)
+
+    def gather(m):
+        out = ybuf[m, mine, :].astype(F32)
+        for g in range(F):
+            for j in range(R):
+                if g or j:
+                    piece(2 * g + m, j).wait_recv()
+                    out = out + xrec[m, g, j].astype(F32)
+        return out
+
+    def give(m, j):
+        buf = (mix, ig)[m].at[mine, :]
+        return remote(buf, buf, ms.at[m, j], mr.at[m, j], {"trow": lax.rem(rr + j, R)})
+
+    def taken(m, j):
+        r = lax.rem(rr + R - j, R)
+        buf = (mix, ig)[m].at[pl.ds(pl.multiple_of(r * TR, TR), TR), :]
+        remote(buf, buf, ms.at[m, j], mr.at[m, j], {"trow": r}).wait_recv()
+
+    loads[0].wait()
+    partial(0)
+    flow(0, 0)
+    loads[1].wait()
+    partial(1)
+    for t in range(1, P - 1):
+        flow(0, t)
+    for k in range(1, K + 1):
+        if k < K:
+            flow(k, 0)
+        final(k - 1)
+        spread(k - 1, 0)
+        if k >= 2:
+            spread(k - 2, P - 1)
+            consume(k - 2)
+        if k + 1 < K:
+            partial(k + 1)
+        for t in range(1, P - 1):
+            if k < K:
+                flow(k, t)
+            spread(k - 1, t)
+    outs = [
+        pltpu.make_async_copy(nrm, nrm_h, out_sem.at[0]),
+        pltpu.make_async_copy(cota, cota_h, out_sem.at[1]),
+        pltpu.make_async_copy(hid, hid_h, out_sem.at[2]),
+    ]
+    for copy in outs:
+        copy.start()
+    mix[mine, :] = (tok[mine, :].astype(F32) + gather(0)).astype(BF)
+    for j in range(1, R):
+        give(0, j).start()
+    spread(K - 1, P - 1)
+    outs.append(pltpu.make_async_copy(dpr, dpr_h, out_sem.at[3]))
+    outs[-1].start()
+    consume(K - 1)
+    dn[...] = gather(1)
+    mean_m, rstd_m = mean_s[mine, 0:1], rstd_s[mine, 0:1]
+    xhat = (tok[mine, :].astype(F32) - mean_m) * rstd_m
+    s1 = jnp.sum(dn[...], axis=1, keepdims=True)
+    s2 = jnp.sum(dn[...] * xhat, axis=1, keepdims=True)
+    lane = lax.broadcasted_iota(jnp.int32, (TR, 128), 1)
+    st2[0] = jnp.where(lane == 0, s1, jnp.where(lane == 1, s2, 0.0))
+    for j in range(1, P):
+        stat(st2, 1, j).start()
+    total = st2[0]
+    for j in range(1, P):
+        stat(st2, 1, j).wait_recv()
+        total = total + st2[j]
+    m1, m2 = total[:, 0:1] / width, total[:, 1:2] / width
+    ig[mine, :] = (
+        cot[mine, :].astype(F32) + rstd_m * (dn[...] - m1 - xhat * m2)
+    ).astype(BF)
+    for j in range(1, R):
+        give(1, j).start()
+    for m in range(2):
+        for j in range(1, R):
+            taken(m, j)
+        outs.append(pltpu.make_async_copy((mix, ig)[m], (mix_h, ig_h)[m], out_sem.at[4 + m]))
+        outs[-1].start()
+
+    for g in range(1, F):
+        share(nrm, 0, g).wait_send()
+        share(cota, 1, g).wait_send()
+    for j in range(1, P):
+        stat(st1, 0, j).wait_send()
+        stat(st2, 1, j).wait_send()
+    for k in range(K):
+        for t in range(P - 1):
+            flow_end(k, t)
+        for d in range(P):
+            spread_end(k, d)
+        for j in range(R):
+            if k // 2 or j:
+                piece(k, j).wait_send()
+    for m in range(2):
+        for j in range(1, R):
+            give(m, j).wait_send()
+    for copy in outs:
+        copy.wait()
+
+
+def fused(F, R, P_, tokens, w_up, w_down, cotangent):
+    T, W = tokens.shape
+    H = w_down.shape[0]
+    K = 2 * F
+    TC, TR = T // P_, T // R
+    S = jax.ShapeDtypeStruct
+    any_spec = pl.BlockSpec(memory_space=pl.ANY)
+    vmem = pl.BlockSpec(memory_space=pltpu.VMEM)
+    dma = pltpu.SemaphoreType.DMA
+    V = pltpu.VMEM
+    mixed, input_gradient, normed, cot_all, hidden, dpre = pl.pallas_call(
+        functools.partial(block_kernel, F, R, P_),
+        out_shape=(
+            S((T, W), BF), S((T, W), BF), S((F * T, W), BF), S((F * T, W), BF),
+            S((F * T, H), BF), S((F * T, H), BF),
+        ),
+        in_specs=[vmem, vmem, any_spec, any_spec],
+        out_specs=(any_spec,) * 6,
+        scratch_shapes=[
+            V(w_up.shape, BF), V(w_down.shape, BF),
+            V((F * T, W), BF), V((F * T, W), BF), V((F * T, H), BF), V((F * T, H), BF),
+            V((K, T, H), BF), V((K, P_, TC, H), BF), V((K, P_, TC, H), BF),
+            V((TC, H), F32), V((TC, H), F32),
+            V((K, T, W), BF), V((2, F, R, TR, W), BF), V((T, W), BF), V((T, W), BF),
+            V((TR, W), F32), V((T, 128), F32), V((T, 128), F32),
+            V((P_, 8, T), F32), V((P_, TR, 128), F32),
+            dma((2,)), dma((6,)), dma((2, F)), dma((2, F)), dma((2, P_)), dma((2, P_)),
+            dma((K, P_)), dma((K, P_)), dma((K, P_)), dma((K, P_)),
+            dma((K, P_)), dma((K, P_)), dma((K, P_)),
+            dma((2, F, R)), dma((2, F, R)), dma((2, R)), dma((2, R)),
+        ],
+        compiler_params=pltpu.CompilerParams(
+            collective_id=0, has_side_effects=True, vmem_limit_bytes=60 * 1024 * 1024
+        ),
+        name="ffn_block",
+    )(tokens, cotangent, w_up, w_down)
+    grad_down = contract(hidden, cot_all, 0, 0).astype(BF)
+    grad_up = contract(normed, dpre, 0, 0).astype(BF)
+    return mixed, input_gradient, grad_up, grad_down
+
+
 def solution(mesh):
+    F, R, P_ = mesh.shape["fsdp"], mesh.shape["trow"], mesh.shape["tcol"]
+    body = functools.partial(fused, F, R, P_) if F * R <= 16 else local
     return jax.shard_map(
-        local,
+        body,
         mesh=mesh,
         in_specs=(
             P("fsdp", "tcol"),

time: 360 us -> 160 us (0.44)
  waiting for transfers between devices: 276 us -> 0 us
  Pallas kernels: 0 us -> 144 us
  blocking collectives: 25.2 us -> 0 us
  matrix products: 33.5 us -> 10.9 us
  between operations: 13.9 us -> 0.67 us
  other arithmetic: 10.2 us -> 0 us
    pallas_call x0 -> x1, Pallas kernels: none -> 144 us  [fused(): pl.pallas_call(functools.partial(block_kernel, F, R, P_), out_shape=(S((T...]
    reduce_scatter x4 -> x0, waiting for transfers between devices: 125 us -> none  [the longest x1 45.6 us: local(): lax.psum_scatter(dhid_part, 'tcol', scatter_dimension=0, tiled=True)]
    all_gather x4 -> x0, waiting for transfers between devices: 120 us -> none  [the longest x1 44.4 us: local(): lax.all_gather(gelu_value(pre).astype(jnp.bfloat16), 'tcol', axis=0, tile...]
    psum x1 -> x0, waiting for transfers between devices: 29.9 us -> none  [local(): branch = lax.psum(branch, 'trow').astype(jnp.float32)]
    psum x2 -> x0, blocking collectives: 25.2 us -> none  [the longest x1 13.5 us: local(): lax.psum((jnp.sum(input_float, axis=1), jnp.sum(input_float * input_float...]
    dot_general x6 -> x2, matrix products: 33.5 us -> 10.9 us  [contract(): lax.dot_general(left, right, (((left_dim,), (right_dim,)), ((), ())), pre...]
    convert_element_type x3 -> x0, other arithmetic: 7.41 us -> none  [the longest x1 2.71 us: local(): (dhid * gelu_slope(pre)).astype(jnp.bfloat16)]
  transfers between devices with their start and end apart: 9 -> 0, of which waited for: 9 -> 0; matrix products, arithmetic and copies ran while one was open for 9% -> 0% of each run, Pallas kernels for 0% -> 0%
where the time goes in v2:
time: 160 us; the launch traced here: 157 us
  Pallas kernels  144 us (90%)
  matrix products  10.9 us (7%)
  local copies, waits for them, and re-layouts  1.6 us (1%)
    pallas_call x1, Pallas kernels, fused(): pl.pallas_call(functools.partial(block_kernel, F, R, P_), out_shape=(S((T...  144 us
    dot_general x2, matrix products, contract(): lax.dot_general(left, right, (((left_dim,), (right_dim,)), ((), ())), pre...  10.9 us

profile of v2, /device:TPU:0, one launch (start us, length us, event | category | flops | bytes accessed | tf_op | source)
XLA Modules:
  0.0 157.5 jit_solution(1197156797494903628)
XLA Ops:
  0.6 144.3 %ffn_block.1 = (bf16[256,1024]{1,0:T(8,128)(2,1)}, bf16[256,1024]{1,0:T(8,128)(2,1)}, bf16[512,1024]{1,0:T(8,128)(2,1)}, bf16[512,1024]{1,0:T(8,128)(2,1)}, bf16...) custom-call(bf16[256,1024]{1,0:T(8,128)(2,1)} %tok.1, bf16[256,1024]{1,0:T(8,128)(2,1)} %cot.1, ...), custom_call_target="tpu_custom_call" | custom-call | tf_op jit(solution)/shard_map/ffn_block/pallas_call | solution.py:436
  145.0 0.0 copy-start.2
  145.0 0.0 copy-start.3
  145.0 6.5 %convolution_convert_fusion.1 = bf16[1024,2048]{1,0:T(8,128)(2,1)} fusion(bf16[512,1024]{1,0:T(8,128)(2,1)} %get-tuple-element.12, bf16[512,2048]{1,0:T(8,128)(2,1)} %get-tuple-element.13), kind=kOutput, calls=%fused_computation.1 | convolution fusion | flops 2149580800 | bytes 7340032 | tf_op jit(solution)/shard_map/dot_general | solution.py:22
  151.5 0.0 copy-done.2
  151.5 0.0 copy-done.3
  151.5 0.0 copy-start.1
  151.5 0.0 copy-start
  151.5 4.4 %convolution_convert_fusion = bf16[2048,1024]{1,0:T(8,128)(2,1)} fusion(bf16[512,2048]{1,0:T(8,128)(2,1)S(1)} %copy-done.2, bf16[512,1024]{1,0:T(8,128)(2,1)S(1)} %copy-done.3), kind=kOutput, calls=%fused_computation | convolution fusion | flops 2149580800 | bytes 7340032 | tf_op jit(solution)/shard_map/dot_general | solution.py:22
  155.9 0.0 copy-done.1
  155.9 0.8 copy.10
  156.7 0.0 copy-done
  156.7 0.8 copy.11
Async XLA Ops:
  145.0 6.5 %copy-start.2 = (bf16[512,2048]{1,0:T(8,128)(2,1)S(1)}, bf16[512,2048]{1,0:T(8,128)(2,1)}, u32[]{:S(2)}) copy-start(bf16[512,2048]{1,0:T(8,128)(2,1)} %get-tuple-element.14) | copy-start | bytes 6291460
  145.0 6.5 %copy-start.3 = (bf16[512,1024]{1,0:T(8,128)(2,1)S(1)}, bf16[512,1024]{1,0:T(8,128)(2,1)}, u32[]{:S(2)}) copy-start(bf16[512,1024]{1,0:T(8,128)(2,1)} %get-tuple-element.15) | copy-start | bytes 3145732
  151.5 4.4 %copy-start.1 = (bf16[256,1024]{1,0:T(8,128)(2,1)S(1)}, bf16[256,1024]{1,0:T(8,128)(2,1)}, u32[]{:S(2)}) copy-start(bf16[256,1024]{1,0:T(8,128)(2,1)} %get-tuple-element.20) | copy-start | bytes 1572868
  151.5 5.2 %copy-start = (bf16[256,1024]{1,0:T(8,128)(2,1)S(1)}, bf16[256,1024]{1,0:T(8,128)(2,1)}, u32[]{:S(2)}) copy-start(bf16[256,1024]{1,0:T(8,128)(2,1)} %get-tuple-element.21) | copy-start | bytes 1572868

commit v3 on v2

--- a/solution.py
+++ b/solution.py
@@ -68,6 +68,7 @@
 
 MESH = pl.DeviceIdType.MESH
 BF, F32 = jnp.bfloat16, jnp.float32
+HALVES, SPACING = 4, 1
 
 
 def block_kernel(
@@ -79,7 +80,10 @@
     T, W = tok.shape
     H = wdn.shape[0]
     TC, TR = T // P, T // R
-    K = 2 * F
+    TS = TC // R
+    HH = H // HALVES
+    rounds = [(g, m, h) for g in range(F) for m in range(2) for h in range(HALVES)]
+    K = len(rounds)
     f, rr, p = lax.axis_index("fsdp"), lax.axis_index("trow"), lax.axis_index("tcol")
     sends = []
 
@@ -145,8 +149,6 @@
 
     for j in range(1, P):
         stat(st1, 0, j).start()
-    for g in range(1, F):
-        share(cota, 1, g).start()
     total = st1[0]
     for j in range(1, P):
         stat(st1, 0, j).wait_recv()
@@ -161,24 +163,29 @@
     nrm[rows(0), :] = ((tok[...].astype(F32) - mean) * rstd).astype(BF)
     for g in range(1, F):
         share(nrm, 0, g).start()
-
-    BN = min(H, 512)
+    for g in range(1, F):
+        share(cota, 1, g).start()
+
+    BN = min(HH, 512)
 
     def partial(k):
-        g, m = k // 2, k % 2
-        if g:
+        g, m, h = rounds[k]
+        if g and not h:
             arrive((nrm, cota)[m], m, F - g)
+        if k == HALVES:
+            loads[1].wait()
 
         def body(i, _):
             n = pl.ds(pl.multiple_of(i * BN, BN), BN)
+            w = pl.ds(pl.multiple_of(h * HH + i * BN, BN), BN)
             if m == 0:
-                out = jnp.dot(nrm[rows(g), :], wup[:, n], preferred_element_type=F32)
+                out = jnp.dot(nrm[rows(g), :], wup[:, w], preferred_element_type=F32)
             else:
-                out = contract(cota[rows(g), :], wdn[n, :], 1, 1)
+                out = contract(cota[rows(g), :], wdn[w, :], 1, 1)
             part[k, :, n] = out.astype(BF)
             return 0
 
-        lax.fori_loop(0, H // BN, body, 0)
+        lax.fori_loop(0, HH // BN, body, 0)
 
     def at(c):
         return pl.ds(pl.multiple_of(c * TC, TC), TC)
@@ -233,7 +240,7 @@
             to_left(k, t - P + 1 + p).wait_send()
 
     def final(k):
-        g, m = k // 2, k % 2
+        g, m, h = rounds[k]
         acc[...] = part[k, at(p), :].astype(F32)
 
         @pl.when(p > 0)
@@ -250,20 +257,24 @@
             n = pl.ds(pl.multiple_of(i * BN, BN), BN)
             a = acc[:, n]
             if m == 0:
-                hid[chunk(g, p), n] = gelu_value(a).astype(BF)
-                slope[:, n] = gelu_slope(a)
+                hid[h, chunk(g, p), n] = gelu_value(a).astype(BF)
+                slope[g, h, :, n] = gelu_slope(a)
             else:
-                dpr[chunk(g, p), n] = (a * slope[:, n]).astype(BF)
+                dpr[h, chunk(g, p), n] = (a * slope[g, h, :, n]).astype(BF)
             return 0
 
-        lax.fori_loop(0, H // BN, body, 0)
+        lax.fori_loop(0, HH // BN, body, 0)
+
+    def passed(k, c):
+        g, m, h = rounds[k]
+        return (hid, dpr)[m].at[h, chunk(g, c), :]
 
     def pass_right(k, c):
-        buf = (hid, dpr)[k % 2].at[chunk(k // 2, c), :]
+        buf = passed(k, c)
         return remote(buf, buf, ag_rs.at[k, c], ag_r.at[k, c], {"tcol": lax.rem(p + 1, P)})
 
     def pass_left(k, c):
-        buf = (hid, dpr)[k % 2].at[chunk(k // 2, c), :]
+        buf = passed(k, c)
         return remote(buf, buf, ag_ls.at[k, c], ag_r.at[k, c], {"tcol": lax.rem(p + P - 1, P)})
 
     def spread(k, d):
@@ -295,111 +306,144 @@
         def _():
             pass_left(k, p + d).wait_send()
 
-    def piece(k, j):
-        g, m = k // 2, k % 2
+    def sub(c, r):
+        return pl.ds(pl.multiple_of(c * TC + r * TS, TS), TS)
+
+    def piece(m, g, j, c):
         r = lax.rem(rr + j, R)
         return remote(
-            ybuf.at[k, pl.ds(pl.multiple_of(r * TR, TR), TR), :], xrec.at[m, g, j],
-            xs.at[m, g, j], xr.at[m, g, j], {"fsdp": group(g), "trow": r},
+            ybuf.at[m, g, sub(c, r), :], xrec.at[m, g, j, c],
+            xs.at[m, g, j, c], xr.at[m, g, j, c], {"fsdp": group(g), "trow": r},
         )
 
     BW = min(W, 256)
 
-    def consume(k):
-        g, m = k // 2, k % 2
+    def project(k, c=None):
+        g, m, _ = rounds[k]
+        src, dst = (rows(g), pl.ds(0, T)) if c is None else (chunk(g, c), at(c))
 
         def body(i, _):
             n = pl.ds(pl.multiple_of(i * BW, BW), BW)
-            if m == 0:
-                out = jnp.dot(hid[rows(g), :], wdn[:, n], preferred_element_type=F32)
-            else:
-                out = contract(dpr[rows(g), :], wup[n, :], 1, 1)
-            ybuf[k, :, n] = out.astype(BF)
+            out = 0.0
+            for h in range(HALVES):
+                w = slice(h * HH, (h + 1) * HH)
+                if m == 0:
+                    out = out + contract(hid[h, src, :], wdn[w, n], 1, 0)
+                else:
+                    out = out + contract(dpr[h, src, :], wup[n, w], 1, 1)
+            ybuf[m, g, dst, n] = out.astype(BF)
             return 0
 
         lax.fori_loop(0, W // BW, body, 0)
         for j in range(R):
             if g or j:
-                piece(k, j).start()
-
-    mine = pl.ds(pl.multiple_of(rr * TR, TR), TR)
-
-    def gather(m):
-        out = ybuf[m, mine, :].astype(F32)
+                for cc in range(P) if c is None else (c,):
+                    piece(m, g, j, cc).start()
+
+    def consume(k):
+        project(k)
+
+    def consume_at(k, d):
+        if d == 0:
+            project(k, p)
+        else:
+            pl.when(p >= d)(lambda: project(k, p - d))
+            pl.when(p + d <= P - 1)(lambda: project(k, p + d))
+
+    def gather(m, c):
+        out = ybuf[m, 0, sub(c, rr), :].astype(F32)
         for g in range(F):
             for j in range(R):
                 if g or j:
-                    piece(2 * g + m, j).wait_recv()
-                    out = out + xrec[m, g, j].astype(F32)
+                    piece(m, g, j, c).wait_recv()
+                    out = out + xrec[m, g, j, c].astype(F32)
         return out
 
-    def give(m, j):
-        buf = (mix, ig)[m].at[mine, :]
-        return remote(buf, buf, ms.at[m, j], mr.at[m, j], {"trow": lax.rem(rr + j, R)})
-
-    def taken(m, j):
+    def give(m, j, c):
+        buf = (mix, ig)[m].at[sub(c, rr), :]
+        return remote(buf, buf, ms.at[m, j, c], mr.at[m, j, c], {"trow": lax.rem(rr + j, R)})
+
+    def taken(m, j, c):
         r = lax.rem(rr + R - j, R)
-        buf = (mix, ig)[m].at[pl.ds(pl.multiple_of(r * TR, TR), TR), :]
-        remote(buf, buf, ms.at[m, j], mr.at[m, j], {"trow": r}).wait_recv()
+        buf = (mix, ig)[m].at[sub(c, r), :]
+        remote(buf, buf, ms.at[m, j, c], mr.at[m, j, c], {"trow": r}).wait_recv()
 
     loads[0].wait()
     partial(0)
-    flow(0, 0)
-    loads[1].wait()
-    partial(1)
-    for t in range(1, P - 1):
-        flow(0, t)
-    for k in range(1, K + 1):
-        if k < K:
-            flow(k, 0)
-        final(k - 1)
-        spread(k - 1, 0)
-        if k >= 2:
-            spread(k - 2, P - 1)
-            consume(k - 2)
-        if k + 1 < K:
-            partial(k + 1)
-        for t in range(1, P - 1):
-            if k < K:
+    last = 2 * (P - 1)
+    ticks = (K - 1) * SPACING + last
+    for tick in range(ticks):
+        for k in reversed(range(K)):
+            t = tick - SPACING * k
+            if 0 <= t <= P - 2:
                 flow(k, t)
-            spread(k - 1, t)
+            elif t == P - 1:
+                final(k)
+                spread(k, 0)
+            elif P - 1 < t <= last:
+                spread(k, t - P + 1)
+            if P - 1 <= t and k == K - 1:
+                consume_at(k, t - P + 1)
+        for k in range(K):
+            if tick + 1 == SPACING * k:
+                partial(k)
+            if tick == SPACING * k + last and rounds[k][2] == HALVES - 1:
+                consume(k)
     outs = [
         pltpu.make_async_copy(nrm, nrm_h, out_sem.at[0]),
         pltpu.make_async_copy(cota, cota_h, out_sem.at[1]),
-        pltpu.make_async_copy(hid, hid_h, out_sem.at[2]),
+    ] + [
+        pltpu.make_async_copy(hid.at[h], hid_h.at[:, pl.ds(h * HH, HH)], out_sem.at[4 + h])
+        for h in range(HALVES)
     ]
     for copy in outs:
         copy.start()
-    mix[mine, :] = (tok[mine, :].astype(F32) + gather(0)).astype(BF)
-    for j in range(1, R):
-        give(0, j).start()
+    for c in range(P):
+        mix[sub(c, rr), :] = (tok[sub(c, rr), :].astype(F32) + gather(0, c)).astype(BF)
+        for j in range(1, R):
+            give(0, j, c).start()
     spread(K - 1, P - 1)
-    outs.append(pltpu.make_async_copy(dpr, dpr_h, out_sem.at[3]))
-    outs[-1].start()
-    consume(K - 1)
-    dn[...] = gather(1)
-    mean_m, rstd_m = mean_s[mine, 0:1], rstd_s[mine, 0:1]
-    xhat = (tok[mine, :].astype(F32) - mean_m) * rstd_m
-    s1 = jnp.sum(dn[...], axis=1, keepdims=True)
-    s2 = jnp.sum(dn[...] * xhat, axis=1, keepdims=True)
-    lane = lax.broadcasted_iota(jnp.int32, (TR, 128), 1)
-    st2[0] = jnp.where(lane == 0, s1, jnp.where(lane == 1, s2, 0.0))
+    consume_at(K - 1, P - 1)
+    for h in range(HALVES):
+        outs.append(
+            pltpu.make_async_copy(
+                dpr.at[h], dpr_h.at[:, pl.ds(h * HH, HH)], out_sem.at[4 + HALVES + h]
+            )
+        )
+        outs[-1].start()
+    lane = lax.broadcasted_iota(jnp.int32, (TS, 128), 1)
+
+    def xhat(c):
+        return (tok[sub(c, rr), :].astype(F32) - mean_s[sub(c, rr), 0:1]) * rstd_s[sub(c, rr), 0:1]
+
+    for c in range(P):
+        d = gather(1, c)
+        dn[c * TS : (c + 1) * TS, :] = d
+        s1 = jnp.sum(d, axis=1, keepdims=True)
+        s2 = jnp.sum(d * xhat(c), axis=1, keepdims=True)
+        st2[0, c * TS : (c + 1) * TS, :] = jnp.where(
+            lane == 0, s1, jnp.where(lane == 1, s2, 0.0)
+        )
     for j in range(1, P):
         stat(st2, 1, j).start()
     total = st2[0]
     for j in range(1, P):
         stat(st2, 1, j).wait_recv()
         total = total + st2[j]
-    m1, m2 = total[:, 0:1] / width, total[:, 1:2] / width
-    ig[mine, :] = (
-        cot[mine, :].astype(F32) + rstd_m * (dn[...] - m1 - xhat * m2)
-    ).astype(BF)
-    for j in range(1, R):
-        give(1, j).start()
+    for c in range(P):
+        block = total[c * TS : (c + 1) * TS]
+        m1, m2 = block[:, 0:1] / width, block[:, 1:2] / width
+        ig[sub(c, rr), :] = (
+            cot[sub(c, rr), :].astype(F32)
+            + rstd_s[sub(c, rr), 0:1] * (dn[c * TS : (c + 1) * TS, :] - m1 - xhat(c) * m2)
+        ).astype(BF)
+        for j in range(1, R):
+            give(1, j, c).start()
     for m in range(2):
         for j in range(1, R):
-            taken(m, j)
-        outs.append(pltpu.make_async_copy((mix, ig)[m], (mix_h, ig_h)[m], out_sem.at[4 + m]))
+            for c in range(P):
+                taken(m, j, c)
+        outs.append(pltpu.make_async_copy((mix, ig)[m], (mix_h, ig_h)[m], out_sem.at[2 + m]))
         outs[-1].start()
 
     for g in range(1, F):
@@ -414,11 +458,14 @@
         for d in range(P):
             spread_end(k, d)
         for j in range(R):
-            if k // 2 or j:
-                piece(k, j).wait_send()
+            g, m, h = rounds[k]
+            if h == 0 and (g or j):
+                for c in range(P):
+                    piece(m, g, j, c).wait_send()
     for m in range(2):
         for j in range(1, R):
-            give(m, j).wait_send()
+            for c in range(P):
+                give(m, j, c).wait_send()
     for copy in outs:
         copy.wait()
 
@@ -426,7 +473,8 @@
 def fused(F, R, P_, tokens, w_up, w_down, cotangent):
     T, W = tokens.shape
     H = w_down.shape[0]
-    K = 2 * F
+    K = 2 * F * HALVES
+    HH = H // HALVES
     TC, TR = T // P_, T // R
     S = jax.ShapeDtypeStruct
     any_spec = pl.BlockSpec(memory_space=pl.ANY)
@@ -443,16 +491,16 @@
         out_specs=(any_spec,) * 6,
         scratch_shapes=[
             V(w_up.shape, BF), V(w_down.shape, BF),
-            V((F * T, W), BF), V((F * T, W), BF), V((F * T, H), BF), V((F * T, H), BF),
-            V((K, T, H), BF), V((K, P_, TC, H), BF), V((K, P_, TC, H), BF),
-            V((TC, H), F32), V((TC, H), F32),
-            V((K, T, W), BF), V((2, F, R, TR, W), BF), V((T, W), BF), V((T, W), BF),
+            V((F * T, W), BF), V((F * T, W), BF), V((HALVES, F * T, HH), BF), V((HALVES, F * T, HH), BF),
+            V((K, T, HH), BF), V((K, P_, TC, HH), BF), V((K, P_, TC, HH), BF),
+            V((TC, HH), F32), V((F, HALVES, TC, HH), F32),
+            V((2, F, T, W), BF), V((2, F, R, P_, TC // R, W), BF), V((T, W), BF), V((T, W), BF),
             V((TR, W), F32), V((T, 128), F32), V((T, 128), F32),
             V((P_, 8, T), F32), V((P_, TR, 128), F32),
-            dma((2,)), dma((6,)), dma((2, F)), dma((2, F)), dma((2, P_)), dma((2, P_)),
+            dma((2,)), dma((4 + 2 * HALVES,)), dma((2, F)), dma((2, F)), dma((2, P_)), dma((2, P_)),
             dma((K, P_)), dma((K, P_)), dma((K, P_)), dma((K, P_)),
             dma((K, P_)), dma((K, P_)), dma((K, P_)),
-            dma((2, F, R)), dma((2, F, R)), dma((2, R)), dma((2, R)),
+            dma((2, F, R, P_)), dma((2, F, R, P_)), dma((2, R, P_)), dma((2, R, P_)),
         ],
         compiler_params=pltpu.CompilerParams(
             collective_id=0, has_side_effects=True, vmem_limit_bytes=60 * 1024 * 1024

time: 160 us -> 154 us (0.963); the launches traced: 157 us -> 154 us
  Pallas kernels: 144 us -> 141 us
    pallas_call x1, Pallas kernels: 144 us -> 141 us  [fused(): pl.pallas_call(functools.partial(block_kernel, F, R, P_), out_shape=(S((T...]
where the time goes in v3:
time: 154 us
  Pallas kernels  141 us (92%)
  matrix products  10.9 us (7%)
  local copies, waits for them, and re-layouts  1.6 us (1%)
    pallas_call x1, Pallas kernels, fused(): pl.pallas_call(functools.partial(block_kernel, F, R, P_), out_shape=(S((T...  141 us
    dot_general x2, matrix products, contract(): lax.dot_general(left, right, (((left_dim,), (right_dim,)), ((), ())), pre...  10.9 us

profile of v3, /device:TPU:0, one launch (start us, length us, event | category | flops | bytes accessed | tf_op | source)
XLA Modules:
  0.0 154.2 jit_solution(15288159752686560690)
XLA Ops:
  0.6 141.1 %ffn_block.1 = (bf16[256,1024]{1,0:T(8,128)(2,1)}, bf16[256,1024]{1,0:T(8,128)(2,1)}, bf16[512,1024]{1,0:T(8,128)(2,1)}, bf16[512,1024]{1,0:T(8,128)(2,1)}, bf16...) custom-call(bf16[256,1024]{1,0:T(8,128)(2,1)} %tok.1, bf16[256,1024]{1,0:T(8,128)(2,1)} %cot.1, ...), custom_call_target="tpu_custom_call" | custom-call | tf_op jit(solution)/shard_map/ffn_block/pallas_call | solution.py:484
  141.7 0.0 copy-start.2
  141.7 0.0 copy-start.3
  141.7 6.5 %convolution_convert_fusion.1 = bf16[1024,2048]{1,0:T(8,128)(2,1)} fusion(bf16[512,1024]{1,0:T(8,128)(2,1)} %get-tuple-element.12, bf16[512,2048]{1,0:T(8,128)(2,1)} %get-tuple-element.13), kind=kOutput, calls=%fused_computation.1 | convolution fusion | flops 2149580800 | bytes 7340032 | tf_op jit(solution)/shard_map/dot_general | solution.py:22
  148.2 0.0 copy-done.2
  148.2 0.0 copy-done.3
  148.2 0.0 copy-start.1
  148.2 0.0 copy-start
  148.2 4.4 %convolution_convert_fusion = bf16[2048,1024]{1,0:T(8,128)(2,1)} fusion(bf16[512,2048]{1,0:T(8,128)(2,1)S(1)} %copy-done.2, bf16[512,1024]{1,0:T(8,128)(2,1)S(1)} %copy-done.3), kind=kOutput, calls=%fused_computation | convolution fusion | flops 2149580800 | bytes 7340032 | tf_op jit(solution)/shard_map/dot_general | solution.py:22
  152.6 0.0 copy-done.1
  152.6 0.8 copy.10
  153.4 0.0 copy-done
  153.4 0.8 copy.11
Async XLA Ops:
  141.7 6.5 %copy-start.2 = (bf16[512,2048]{1,0:T(8,128)(2,1)S(1)}, bf16[512,2048]{1,0:T(8,128)(2,1)}, u32[]{:S(2)}) copy-start(bf16[512,2048]{1,0:T(8,128)(2,1)} %get-tuple-element.14) | copy-start | bytes 6291460
  141.7 6.5 %copy-start.3 = (bf16[512,1024]{1,0:T(8,128)(2,1)S(1)}, bf16[512,1024]{1,0:T(8,128)(2,1)}, u32[]{:S(2)}) copy-start(bf16[512,1024]{1,0:T(8,128)(2,1)} %get-tuple-element.15) | copy-start | bytes 3145732
  148.2 4.4 %copy-start.1 = (bf16[256,1024]{1,0:T(8,128)(2,1)S(1)}, bf16[256,1024]{1,0:T(8,128)(2,1)}, u32[]{:S(2)}) copy-start(bf16[256,1024]{1,0:T(8,128)(2,1)} %get-tuple-element.20) | copy-start | bytes 1572868
  148.2 5.2 %copy-start = (bf16[256,1024]{1,0:T(8,128)(2,1)S(1)}, bf16[256,1024]{1,0:T(8,128)(2,1)}, u32[]{:S(2)}) copy-start(bf16[256,1024]{1,0:T(8,128)(2,1)} %get-tuple-element.21) | copy-start | bytes 1572868
